TPU v7x, 512 devices: a whole 4x4x16 slice. The times are simulated.
512 devices in a mesh: frames: 32 (over y, x, core), heads: 16 (over z).
Axes of the slice: x: 4, y: 4, z: 16, core: 2. Of those that a mesh axis runs over, the one named last changes fastest.
Arguments:
- frames: bfloat16 [32768, 1152], P('frames', 'heads'), may hold values from -6 to 6
- latents: bfloat16 [256, 1152], P('frames'), may hold values from -400 to 400
- w_query: bfloat16 [1152, 4096], P(None, 'heads'), may hold values from -0.1875 to 0.1875
- w_key: bfloat16 [1152, 4096], P(None, 'heads'), may hold values from -0.1875 to 0.1875
- w_value: bfloat16 [1152, 4096], P(None, 'heads'), may hold values from -0.1875 to 0.1875
- w_out: bfloat16 [4096, 8192], P('heads', 'frames'), may hold values from -0.09375 to 0.09375
- norm_gain: float32 [8192], P('frames'), may hold values from 0.5 to 1.5
- w_gate: bfloat16 [8192, 16384], P('frames', 'heads'), may hold values from -0.0625 to 0.0625
- w_up: bfloat16 [8192, 16384], P('frames', 'heads'), may hold values from -0.0625 to 0.0625
- w_down: bfloat16 [16384, 8192], P('heads', 'frames'), may hold values from -0.046875 to 0.046875
Outputs:
- block_out: bfloat16 [256, 8192], P('heads', 'frames')
All inputs are finite; a program needn't handle non-finite values.
Results may differ from a plain program's by a relative error of at most 0.023.
Values may be sent and summed in bfloat16 or wider, within the bound.
No kernel may reach another device: no remote copies, remote signals or barrier semaphores. Data moves between devices by JAX's collectives and lax.ppermute only.
A program may use at most 64 MiB of HBM per device.

v0:
```python
import jax
import jax.numpy as jnp
from jax import lax
from jax.sharding import Mesh
from jax.sharding import PartitionSpec as P

HDIM = 128
D = 8192
FRAMES = ("frames_0", "frames_1", "frames_2")


norm_eps = 1e-06


def in_order(blocks, dim):
    blocks = jnp.moveaxis(blocks, 0, dim)
    lengths = blocks.shape
    return blocks.reshape(*lengths[:dim], lengths[dim] * lengths[dim + 1], *lengths[dim + 2 :])


def sent_to_all(array, axis):
    peers = lax.axis_size(axis)
    return lax.all_to_all(
        jnp.broadcast_to(array[None], (peers, *array.shape)), axis, 0, 0, tiled=True
    )


def collect(array, axis, dim):
    return in_order(sent_to_all(array, axis), dim)


def merged_by_axis(array, axes, combine):
    for axis in axes:
        pieces = jax.tree.map(lambda part: lax.all_gather(part, axis), array)
        array = jax.tree.map(lambda part: part[0], pieces)
        for k in range(1, lax.axis_size(axis)):
            array = combine(array, jax.tree.map(lambda part: part[k], pieces))
    return array


def cut_along(array, dim, peers):
    lengths = array.shape
    blocks = array.reshape(*lengths[:dim], peers, lengths[dim] // peers, *lengths[dim + 1 :])
    return jnp.moveaxis(blocks, dim, 0)


def sum_at_owner(array, axis, dim):
    blocks = cut_along(array, dim, lax.axis_size(axis))
    arrived = lax.all_to_all(blocks, axis, split_axis=0, concat_axis=0, tiled=True)
    return arrived.sum(axis=0)


def of_everyone(array, axis):
    everything = sent_to_all(array, axis)
    return jnp.sum(everything, axis=0)


def sum_packed(arrays, axis, dims):
    peers = lax.axis_size(axis)
    blocks = [cut_along(a, dim, peers) for a, dim in zip(arrays, dims)]
    lines = jnp.concatenate([b.reshape(peers, -1) for b in blocks], axis=1)
    width = max(16, -(-lines.shape[1] // 1024) * 8)
    lines = jnp.pad(lines, ((0, 0), (0, width * 128 - lines.shape[1]))).reshape(-1, 128)
    line, at, finished = (lax.psum_scatter(lines, axis, tiled=True).reshape(-1), 0, [])
    for b in blocks:
        part = b[0]
        finished.append(line[at : at + part.size].reshape(part.shape))
        at += part.size
    return tuple(finished)


def combine_parts(first, second):
    first_max, first_total, first_mixed = first
    second_max, second_total, second_mixed = second
    joined_max = jnp.maximum(first_max, second_max)
    first_scale = jnp.exp(first_max - joined_max)
    second_scale = jnp.exp(second_max - joined_max)
    joined_total = first_total * first_scale + second_total * second_scale
    joined_mixed = first_mixed * first_scale[:, :, None] + second_mixed * second_scale[:, :, None]
    return (joined_max, joined_total, joined_mixed)


def on_device(frames, latents, w_query, w_key, w_value, w_out, norm_gain, w_gate, w_up, w_down):
    local_query = jnp.dot(latents, w_query, preferred_element_type=jnp.float32).astype(jnp.bfloat16)
    queries = collect(local_query, FRAMES, 0)
    width = w_key.shape[1]
    piece = lax.all_gather(frames, "heads", axis=1, tiled=True)
    keys = jnp.dot(piece, w_key, preferred_element_type=jnp.float32)
    values = jnp.dot(piece, w_value, preferred_element_type=jnp.float32)
    heads_here = width // HDIM
    latent_count = queries.shape[0]
    query_heads = queries.reshape(latent_count, heads_here, HDIM)
    key_heads = keys.astype(jnp.bfloat16).reshape(-1, heads_here, HDIM)
    value_heads = values.astype(jnp.bfloat16).reshape(-1, heads_here, HDIM)
    scores = jnp.einsum(
        "qhd,khd->qhk", query_heads, key_heads, preferred_element_type=jnp.float32
    ) * HDIM ** (-0.5)
    local_max = jnp.max(scores, axis=2)
    weights = jnp.exp(scores - local_max[:, :, None])
    total = jnp.sum(weights, axis=2)
    mixed = jnp.einsum(
        "qhk,khd->qhd",
        weights.astype(jnp.bfloat16),
        value_heads,
        preferred_element_type=jnp.float32,
    )
    total, mixed = (total, mixed)
    merged = merged_by_axis((local_max, total, mixed), FRAMES, combine_parts)
    attention = (
        (merged[2] / merged[1][:, :, None]).reshape(latent_count, width).astype(jnp.bfloat16)
    )
    latent_state = sum_at_owner(
        jnp.dot(attention, w_out, preferred_element_type=jnp.float32), "heads", 0
    ).astype(jnp.bfloat16)
    latent_full = collect(latent_state, "heads", 0)
    full_float = latent_full.astype(jnp.float32)
    square_part = jnp.sum(full_float * full_float, axis=1)
    normed = (full_float * norm_gain[None, :]).astype(jnp.bfloat16)
    gate_part = jnp.dot(normed, w_gate, preferred_element_type=jnp.float32)
    up_part = jnp.dot(normed, w_up, preferred_element_type=jnp.float32)
    squares = of_everyone(square_part, FRAMES)
    gate_sum, up_sum = sum_packed((gate_part, up_part), FRAMES, (0, 0))
    share_rows = gate_sum.shape[0]
    square_rows = lax.dynamic_slice_in_dim(
        squares, lax.axis_index(FRAMES) * share_rows, share_rows, 0
    )
    scale_rows = lax.rsqrt(square_rows / D + norm_eps)[:, None]
    hidden = (jax.nn.silu(gate_sum * scale_rows) * (up_sum * scale_rows)).astype(jnp.bfloat16)
    hidden_full = collect(hidden, FRAMES, 0)
    down = sum_at_owner(
        jnp.dot(hidden_full, w_down, preferred_element_type=jnp.float32), "heads", 0
    )
    return (latent_state.astype(jnp.float32) + down).astype(jnp.bfloat16)


def solution(mesh):
    torus = Mesh(
        mesh.devices.reshape(4, 4, 2, mesh.shape["heads"]),
        ("frames_0", "frames_1", "frames_2", "heads"),
    )
    placed = (
        P(FRAMES, "heads"),
        P(FRAMES, None),
        P(None, "heads"),
        P(None, "heads"),
        P(None, "heads"),
        P("heads", FRAMES),
        P(FRAMES),
        P(FRAMES, "heads"),
        P(FRAMES, "heads"),
        P("heads", FRAMES),
    )
    return jax.shard_map(
        on_device, mesh=torus, in_specs=placed, out_specs=P("heads", FRAMES), check_vma=False
    )
```

profile of v0, /device:TPU:32, one launch (start us, length us, event | category | flops | bytes accessed | tf_op | source)
XLA Modules:
  0.0 375.0 jit_solution(16356984806654069798)
XLA Ops:
  6.5 0.7 all-gather.7.cloned.1.call-update
  7.3 1.3 convolution_convert_fusion.2
  8.6 14.9 %all_to_all.31 = bf16[32,8,256]{2,1,0:T(8,128)(2,1)S(1)} all-to-all(bf16[32,8,256]{2,1,0:T(8,128)(2,1)S(1)} %broadcast_in_dim.10), channel_id=1, replica_groups=mesh['frames_0'=4,'frames_1'=4,'frames_2'=2,'heads'=16] {'frames_0','fra..., dimensions={0} | all-to-all | bytes 262144 | tf_op jit(solution)/shard_map/all_to_all | solution.py:23
  23.5 63.2 %all-gather.7.cloned.1.call-done = bf16[1024,1152]{0,1:T(8,128)(2,1)} async-done(((bf16[1024,72]{0,1:T(8,128)(2,1)}), bf16[1024,1152]{0,1:T(8,128)(2,1)}) %all-gather.7.cloned.1.call-update) | async-done | bytes 2359312 | tf_op jit(solution)/shard_map/all_gather | solution.py:87
  86.7 2.6 convolution_convert_fusion
  89.9 1.1 copy-done.6
  91.0 0.9 convolution_convert_fusion.1
  91.9 1.2 convolution_bitcast_fusion
  93.2 11.1 %all-gather.1 = f32[1024,2]{0,1:T(2,128)S(1)} all-gather(f32[256,2]{0,1:T(2,128)S(1)} %get-tuple-element.30), channel_id=3, replica_groups=mesh['frames_0'=4,'frames_1'=4,'frames_2'=2,'heads'=16] {'frames_0'}, dimensions={0}, use_global_device_ids=true | all-gather | bytes 10240 | tf_op jit(solution)/shard_map/all_gather | solution.py:34
  104.4 17.8 %all-gather.11.cloned.1.call-done = f32[1024,2,128]{0,2,1:T(8,128)} async-done(((f32[256,2,128]{0,2,1:T(8,128)}), f32[1024,2,128]{0,2,1:T(8,128)}) %all-gather.11.cloned.1.call-update) | async-done | bytes 1048592 | tf_op jit(solution)/shard_map/all_gather | solution.py:34
  122.2 1.3 fusion.14
  123.4 0.8 copy.47
  124.7 10.4 %all-gather.2 = f32[1024,2]{0,1:T(2,128)S(1)} all-gather(f32[256,2]{0,1:T(2,128)S(1)} %fusion.1), channel_id=4, replica_groups=mesh['frames_0'=4,'frames_1'=4,'frames_2'=2,'heads'=16] {'frames_0'}, dimensions={0}, use_global_device_ids=true | all-gather | bytes 10240 | tf_op jit(solution)/shard_map/all_gather | solution.py:34
  135.2 11.1 %all_gather.56 = f32[4,256,2]{1,2,0:T(2,128)S(1)} all-gather(f32[1,256,2]{1,2,0:T(2,128)S(1)} %get-tuple-element.14), channel_id=1, replica_groups=mesh['frames_0'=4,'frames_1'=4,'frames_2'=2,'heads'=16] {'frames_1'}, dimensions={0}, use_global_device_ids=true | all-gather | bytes 10240 | tf_op jit(solution)/shard_map/all_gather | solution.py:34
  146.3 10.4 %all_gather.51 = f32[4,256,2]{1,2,0:T(2,128)S(1)} all-gather(f32[1,256,2]{1,2,0:T(2,128)S(1)} %get-tuple-element.15), channel_id=1, replica_groups=mesh['frames_0'=4,'frames_1'=4,'frames_2'=2,'heads'=16] {'frames_1'}, dimensions={0}, use_global_device_ids=true | all-gather | bytes 10240 | tf_op jit(solution)/shard_map/all_gather | solution.py:34
  156.8 1.8 all_gather.57
  158.6 1.8 all_gather.53
  162.6 1.7 fusion.8
  164.3 2.3 all_gather.52
  167.8 30.8 %all_to_all.32 = f32[16,16,256]{2,1,0:T(8,128)S(1)} all-to-all(f32[16,16,256]{2,1,0:T(8,128)S(1)} %fusion.23), channel_id=1, replica_groups=mesh['frames_0'=4,'frames_1'=4,'frames_2'=2,'heads'=16] {'heads'}, dimensions={0} | all-to-all | bytes 524288 | tf_op jit(solution)/shard_map/all_to_all | solution.py:49
  198.7 20.4 %all_to_all.33 = bf16[16,16,256]{2,1,0:T(8,128)(2,1)S(1)} all-to-all(bf16[16,16,256]{2,1,0:T(8,128)(2,1)S(1)} %broadcast_in_dim.11), channel_id=1, replica_groups=mesh['frames_0'=4,'frames_1'=4,'frames_2'=2,'heads'=16] {'heads'}, dimensions={0} | all-to-all | bytes 262144 | tf_op jit(solution)/shard_map/all_to_all | solution.py:23
  219.4 1.2 reshape_reshape.11
  220.9 1.2 reshape_reshape.10
  222.1 1.7 pad_maximum_fusion
  223.7 1.5 reshape.311
  225.5 0.6 broadcast_in_dim.13
  226.1 6.0 %all-to-all-start.3 = ((f32[32,1,256]{2,1,0:T(1,128)}), f32[32,1,256]{2,1,0:T(1,128)S(1)}, u32[]{:S(2)}, u32[]{:S(2)}) async-start(f32[32,1,256]{2,1,0:T(1,128)} %broadcast_in_dim.13), calls=%async_computation.4 | async-start | bytes 65536 | tf_op jit(solution)/shard_map/all_to_all | solution.py:23
  232.1 7.4 %all-to-all-done.3 = f32[32,1,256]{2,1,0:T(1,128)S(1)} async-done(((f32[32,1,256]{2,1,0:T(1,128)}), f32[32,1,256]{2,1,0:T(1,128)S(1)}, u32[]{:S(2)}, u32[]{:S(2)}) %all-to-all-start.3) | async-done | bytes 32800 | tf_op jit(solution)/shard_map/all_to_all | solution.py:23
  239.6 79.5 %reduce-scatter.2.cloned.1.call-done = f32[128,128]{1,0:T(8,128)} async-done(((f32[4096,128]{1,0:T(8,128)}), f32[128,128]{1,0:T(8,128)}) %reduce-scatter.2.cloned.1.call-update) | async-done | bytes 65552 | tf_op jit(solution)/shard_map/reduce_scatter | solution.py:64
  319.1 0.8 fusion.63
  320.1 16.6 %all_to_all.34 = bf16[32,8,1024]{2,1,0:T(8,128)(2,1)S(1)} all-to-all(bf16[32,8,1024]{2,1,0:T(8,128)(2,1)S(1)} %broadcast_in_dim.14), channel_id=1, replica_groups=mesh['frames_0'=4,'frames_1'=4,'frames_2'=2,'heads'=16] {'frames_0','fra..., dimensions={0} | all-to-all | bytes 1048576 | tf_op jit(solution)/shard_map/all_to_all | solution.py:23
  337.1 30.8 %all_to_all.35 = f32[16,16,256]{2,1,0:T(8,128)S(1)} all-to-all(f32[16,16,256]{2,1,0:T(8,128)S(1)} %fusion.6), channel_id=1, replica_groups=mesh['frames_0'=4,'frames_1'=4,'frames_2'=2,'heads'=16] {'heads'}, dimensions={0} | all-to-all | bytes 524288 | tf_op jit(solution)/shard_map/all_to_all | solution.py:49
  (65 shorter events, 6.5 us)
Async XLA Ops:
  6.5 80.2 %copy-start = (bf16[1152,256]{1,0:T(8,128)(2,1)S(1)}, bf16[1152,256]{1,0:T(8,128)(2,1)}, u32[]{:S(2)}) copy-start(bf16[1152,256]{1,0:T(8,128)(2,1)} %param.13) | copy-start | bytes 1769476
  6.5 80.2 %all-gather.7.cloned.1.call-start = ((), (), s32[]{:S(2)}) async-start(), calls=%async_computation.7 | async-start | bytes 2506752 | tf_op jit(solution)/shard_map/all_gather | solution.py:87
  7.3 114.9 %all-gather.11.cloned.1.call-start = ((), (), s32[]{:S(2)}) async-start(), calls=%async_computation.10 | async-start | bytes 1310720 | tf_op jit(solution)/shard_map/all_gather | solution.py:34
  86.7 3.1 copy-start.7
  89.3 1.7 copy-start.6
  93.1 69.5 %all-gather.9.cloned.1.call-start = ((), (), s32[]{:S(2)}) async-start(), calls=%async_computation.8 | async-start | bytes 1310720 | tf_op jit(solution)/shard_map/all_gather | solution.py:34
  124.3 194.8 %reduce-scatter.2.cloned.1.call-start = ((), (), s32[]{:S(2)}) async-start(), calls=%async_computation.9 | async-start | bytes 2162688 | tf_op jit(solution)/shard_map/reduce_scatter | solution.py:64
  164.3 3.3 copy-start.4
  167.1 52.0 %copy-start.5 = (f32[256]{0:T(256)S(1)}, f32[256]{0:T(256)}, u32[]{:S(2)}) copy-start(f32[256]{0:T(256)} %param.16) | copy-start | bytes 3076
  167.1 52.0 %copy-start.1 = (bf16[256,1024]{1,0:T(8,128)(2,1)S(1)}, bf16[256,1024]{1,0:T(8,128)(2,1)}, u32[]{:S(2)}) copy-start(bf16[256,1024]{1,0:T(8,128)(2,1)} %param.18) | copy-start | bytes 1572868
  219.1 1.5 copy-start.2
  225.3 111.5 %copy-start.3 = (bf16[1024,256]{1,0:T(8,128)(2,1)S(1)}, bf16[1024,256]{1,0:T(8,128)(2,1)}, u32[]{:S(2)}) copy-start(bf16[1024,256]{1,0:T(8,128)(2,1)} %param.19) | copy-start | bytes 1572868
  226.1 13.4 %all-to-all-start.3 = ((f32[32,1,256]{2,1,0:T(1,128)}), f32[32,1,256]{2,1,0:T(1,128)S(1)}, u32[]{:S(2)}, u32[]{:S(2)}) async-start(f32[32,1,256]{2,1,0:T(1,128)} %broadcast_in_dim.13), calls=%async_computation.4 | async-start | bytes 65536 | tf_op jit(solution)/shard_map/all_to_all | solution.py:23
Sparse Core Ops, SparseCore 0:
  9.4 77.2 all-gather.6
  93.3 28.8 all-gather.10
  124.4 32.1 all-gather.8
  225.4 93.6 reduce-scatter.1
where the time goes:
time: 376 us; the launch traced here: 375 us
  waiting for transfers between devices  169 us (45%)
  blocking collectives  163 us (43%)
  between operations  13.5 us (4%)
  local copies, waits for them, and re-layouts  10.4 us (3%)
  matrix products  7.6 us (2%)
  starting transfers between devices  6.09 us (2%)
  other arithmetic  6.09 us (2%)
    reduce_scatter x1, waiting for transfers between devices, sum_packed(): lax.psum_scatter(lines, axis, tiled=True).reshape(-1)  79.5 us
    all_gather x1, waiting for transfers between devices, on_device(): piece = lax.all_gather(frames, 'heads', axis=1, tiled=True)  63.2 us
    all_to_all x2, blocking collectives, sum_at_owner(): lax.all_to_all(blocks, axis, split_axis=0, concat_axis=0, tiled=True)  61.6 us
    all_to_all x3, blocking collectives, sent_to_all(): lax.all_to_all(jnp.broadcast_to(array[None], (peers, *array.shape)), axis...  51.9 us
    all_gather x7, blocking collectives, merged_by_axis(): pieces = jax.tree.map(lambda part: lax.all_gather(part, axis), array)  49.1 us
    all_gather x2, waiting for transfers between devices, merged_by_axis(): pieces = jax.tree.map(lambda part: lax.all_gather(part, axis), array)  17.8 us
  transfers between devices with their start and end apart: 5, of which 4 were waited for; matrix products, arithmetic and copies ran while one was open for 1% of the time, Pallas kernels for 0%

commit v1 on v0

v1 whole, which is shorter than its diff:
```python
import jax
import jax.numpy as jnp
from jax import lax
from jax.sharding import Mesh
from jax.sharding import PartitionSpec as P

HDIM = 128
D = 8192
FRAMES = ("frames_0", "frames_1", "frames_2")
BF16 = jnp.bfloat16
F32 = jnp.float32


norm_eps = 1e-06


def exchange(blocks, axis):
    return lax.all_to_all(blocks, axis, split_axis=0, concat_axis=0, tiled=True)


def collect_rows(array, axis):
    peers = lax.axis_size(axis)
    blocks = exchange(jnp.broadcast_to(array[None], (peers, *array.shape)), axis)
    return blocks.reshape(peers * array.shape[0], *array.shape[1:])


def sum_rows_at_owner(array, axis):
    peers = lax.axis_size(axis)
    blocks = array.astype(BF16).reshape(peers, array.shape[0] // peers, *array.shape[1:])
    return jnp.sum(exchange(blocks, axis).astype(F32), axis=0)


def split_terms(array, count):
    terms = []
    for _ in range(count):
        term = lax.reduce_precision(array, 8, 7)
        terms.append(term.astype(BF16))
        array = array - term
    return terms


def joined_terms(terms):
    array = terms[-1].astype(F32)
    for term in terms[-2::-1]:
        array = array + term.astype(F32)
    return array


def merged_softmax(local_max, total, mixed):
    peers = lax.axis_size(FRAMES)
    rows, heads = local_max.shape
    share = rows // peers
    terms = jnp.stack(split_terms(local_max, 3) + split_terms(total, 3), axis=-1)
    stats = terms.reshape(peers, share * heads * 6)
    stats = jnp.pad(stats, ((0, 0), (0, -stats.shape[1] % HDIM))).reshape(peers, -1, HDIM)
    body = mixed.astype(BF16).reshape(peers, share * heads, HDIM)
    arrived = exchange(jnp.concatenate([body, stats], axis=1), FRAMES)
    body = arrived[:, : share * heads].reshape(peers, share, heads, HDIM).astype(F32)
    stats = arrived[:, share * heads :].reshape(peers, -1)[:, : share * heads * 6]
    stats = stats.reshape(peers, share, heads, 6)
    part_max = joined_terms([stats[..., k] for k in range(3)])
    part_total = joined_terms([stats[..., k] for k in range(3, 6)])
    scale = jnp.exp(part_max - jnp.max(part_max, axis=0))
    total = jnp.sum(part_total * scale, axis=0)
    mixed = jnp.sum(body * scale[..., None], axis=0)
    return (mixed / total[..., None]).reshape(share, heads * HDIM).astype(BF16)


def on_device(frames, latents, w_query, w_key, w_value, w_out, norm_gain, w_gate, w_up, w_down):
    local_query = jnp.dot(latents, w_query, preferred_element_type=F32).astype(BF16)
    queries = collect_rows(local_query, FRAMES)
    width = w_key.shape[1]
    piece = lax.all_gather(frames, "heads", axis=1, tiled=True)
    keys = jnp.dot(piece, w_key, preferred_element_type=F32)
    values = jnp.dot(piece, w_value, preferred_element_type=F32)
    heads_here = width // HDIM
    latent_count = queries.shape[0]
    query_heads = queries.reshape(latent_count, heads_here, HDIM)
    key_heads = keys.astype(BF16).reshape(-1, heads_here, HDIM)
    value_heads = values.astype(BF16).reshape(-1, heads_here, HDIM)
    scores = jnp.einsum(
        "qhd,khd->qhk", query_heads, key_heads, preferred_element_type=F32
    ) * HDIM ** (-0.5)
    local_max = jnp.max(scores, axis=2)
    weights = jnp.exp(scores - local_max[:, :, None])
    total = jnp.sum(weights, axis=2)
    mixed = jnp.einsum("qhk,khd->qhd", weights.astype(BF16), value_heads, preferred_element_type=F32)
    attention = collect_rows(merged_softmax(local_max, total, mixed), FRAMES)
    latent_state = sum_rows_at_owner(
        jnp.dot(attention, w_out, preferred_element_type=F32), "heads"
    ).astype(BF16)
    latent_full = collect_rows(latent_state, "heads")
    full_float = latent_full.astype(F32)
    square_part = jnp.sum(full_float * full_float, axis=1)
    normed = (full_float * norm_gain[None, :]).astype(BF16)
    gate_part = jnp.dot(normed, w_gate, preferred_element_type=F32).astype(BF16)
    up_part = jnp.dot(normed, w_up, preferred_element_type=F32).astype(BF16)
    square_terms = jnp.stack(split_terms(square_part, 2), axis=1)
    square_terms = jnp.pad(square_terms, ((0, 0), (0, 126)))
    peers = lax.axis_size(FRAMES)
    packed = jnp.concatenate([gate_part, up_part, square_terms], axis=1)
    sums = jnp.sum(exchange(packed.reshape(peers, -1, packed.shape[1]), FRAMES).astype(F32), axis=0)
    units = w_gate.shape[1]
    gate_sum, up_sum = sums[:, :units], sums[:, units : 2 * units]
    squares = sums[:, 2 * units : 2 * units + 1] + sums[:, 2 * units + 1 : 2 * units + 2]
    scale_rows = lax.rsqrt(squares / D + norm_eps)
    hidden = (jax.nn.silu(gate_sum * scale_rows) * (up_sum * scale_rows)).astype(BF16)
    hidden_full = collect_rows(hidden, FRAMES)
    down = sum_rows_at_owner(jnp.dot(hidden_full, w_down, preferred_element_type=F32), "heads")
    return (latent_state.astype(F32) + down).astype(BF16)


def solution(mesh):
    torus = Mesh(
        mesh.devices.reshape(4, 4, 2, mesh.shape["heads"]),
        ("frames_0", "frames_1", "frames_2", "heads"),
    )
    placed = (
        P(FRAMES, "heads"),
        P(FRAMES, None),
        P(None, "heads"),
        P(None, "heads"),
        P(None, "heads"),
        P("heads", FRAMES),
        P(FRAMES),
        P(FRAMES, "heads"),
        P(FRAMES, "heads"),
        P("heads", FRAMES),
    )
    return jax.shard_map(
        on_device, mesh=torus, in_specs=placed, out_specs=P("heads", FRAMES), check_vma=False
    )
```

time: 376 us -> 227 us (0.60)
  waiting for transfers between devices: 169 us -> 63.9 us
  blocking collectives: 163 us -> 138 us
  local copies, waits for them, and re-layouts: 10.4 us -> 2.1 us
  starting transfers between devices: 6.09 us -> 0.01 us
    reduce_scatter x1 -> x0, waiting for transfers between devices: 79.5 us -> none  [sum_packed(): lax.psum_scatter(lines, axis, tiled=True).reshape(-1)]
    all_gather x7 -> x0, blocking collectives: 49.1 us -> none  [merged_by_axis(): pieces = jax.tree.map(lambda part: lax.all_gather(part, axis), array)]
    all_to_all x5 -> x8, blocking collectives: 114 us -> 138 us  [exchange(): return lax.all_to_all(blocks, axis, split_axis=0, concat_axis=0, tiled=True)]
    all_gather x2 -> x0, waiting for transfers between devices: 17.8 us -> none  [merged_by_axis(): pieces = jax.tree.map(lambda part: lax.all_gather(part, axis), array)]
    all_to_all x1 -> x0, waiting for transfers between devices: 7.4 us -> none  [sent_to_all(): lax.all_to_all(jnp.broadcast_to(array[None], (peers, *array.shape)), axis...]
    all_to_all x1 -> x0, starting transfers between devices: 5.97 us -> none  [sent_to_all(): lax.all_to_all(jnp.broadcast_to(array[None], (peers, *array.shape)), axis...]
  transfers between devices with their start and end apart: 5 -> 1, of which waited for: 4 -> 1; matrix products, arithmetic and copies ran while one was open for 1% -> 1% of each run, Pallas kernels for 0% -> 0%
where the time goes in v1:
time: 227 us
  blocking collectives  138 us (61%)
  waiting for transfers between devices  63.9 us (28%)
  between operations  13.7 us (6%)
  matrix products  6.78 us (3%)
  other arithmetic  2.38 us (1%)
    all_to_all x8, blocking collectives, exchange(): return lax.all_to_all(blocks, axis, split_axis=0, concat_axis=0, tiled=True)  138 us
    all_gather x1, waiting for transfers between devices, on_device(): piece = lax.all_gather(frames, 'heads', axis=1, tiled=True)  63.2 us
  transfers between devices with their start and end apart: 1, of which 1 were waited for; matrix products, arithmetic and copies ran while one was open for 1% of the time, Pallas kernels for 0%

profile of v1, /device:TPU:32, one launch (start us, length us, event | category | flops | bytes accessed | tf_op | source)
XLA Modules:
  0.0 226.5 jit_solution(6184290056534508303)
XLA Ops:
  6.5 0.7 all-gather.2.cloned.1.call-update
  7.3 1.3 convolution_convert_fusion.7
  8.6 14.9 %all_to_all.40 = bf16[32,8,256]{2,1,0:T(8,128)(2,1)S(1)} all-to-all(bf16[32,8,256]{2,1,0:T(8,128)(2,1)S(1)} %broadcast_in_dim.8), channel_id=1, replica_groups=mesh['frames_0'=4,'frames_1'=4,'frames_2'=2,'heads'=16] {'frames_0','fra..., dimensions={0} | all-to-all | bytes 262144 | tf_op jit(solution)/shard_map/all_to_all | solution.py:18
  23.5 63.2 %all-gather.2.cloned.1.call-done = bf16[1024,1152]{0,1:T(8,128)(2,1)} async-done(((bf16[1024,72]{0,1:T(8,128)(2,1)}), bf16[1024,1152]{0,1:T(8,128)(2,1)}) %all-gather.2.cloned.1.call-update) | async-done | bytes 2359312 | tf_op jit(solution)/shard_map/all_gather | solution.py:73
  86.7 2.5 %convolution_convert_fusion.2 = bf16[1024,256]{0,1:T(8,128)(2,1)S(1)} fusion(bf16[1024,1152]{0,1:T(8,128)(2,1)} %all-gather.2.cloned.1.call-done, bf16[1152,256]{1,0:T(8,128)(2,1)S(1)} %copy-done), kind=kOutput, calls=%fused_computation.10 | convolution fusion | flops 604241920 | bytes 3473408 | tf_op jit(solution)/shard_map/dot_general | solution.py:74
  89.3 0.5 bitcast_reduce_fusion
  89.8 0.4 fusion.2
  90.2 0.8 copy-done.6
  90.9 0.1 copy-done.7
  91.0 0.9 convolution_convert_fusion.3
  92.0 0.5 fusion.4
  92.5 0.1 copy.82
  92.7 0.2 copy.83
  92.9 0.2 reshape.184
  93.1 15.2 %all_to_all.41 = bf16[32,17,128]{2,1,0:T(8,128)(2,1)S(1)} all-to-all(bf16[32,17,128]{2,1,0:T(8,128)(2,1)S(1)} %pad_maximum_fusion), channel_id=1, replica_groups=mesh['frames_0'=4,'frames_1'=4,'frames_2'=2,'heads'=16] {'frames_0','fra..., dimensions={0} | all-to-all | bytes 278528 | tf_op jit(solution)/shard_map/all_to_all | solution.py:18
  108.5 0.1 fusion.32
  108.7 0.2 fusion.20
  109.0 0.1 multiply_reduce_fusion.1
  109.3 11.4 %all_to_all.42 = bf16[32,8,256]{2,1,0:T(8,128)(2,1)S(1)} all-to-all(bf16[32,8,256]{2,1,0:T(8,128)(2,1)S(1)} %broadcast_in_dim.9), channel_id=1, replica_groups=mesh['frames_0'=4,'frames_1'=4,'frames_2'=2,'heads'=16] {'frames_0','fra..., dimensions={0} | all-to-all | bytes 262144 | tf_op jit(solution)/shard_map/all_to_all | solution.py:18
  120.7 0.2 convolution_convert_fusion.5
  120.9 22.1 %all_to_all.43 = bf16[16,16,256]{2,1,0:T(8,128)(2,1)S(1)} all-to-all(bf16[16,16,256]{2,1,0:T(8,128)(2,1)S(1)} %bitcast.85), channel_id=1, replica_groups=mesh['frames_0'=4,'frames_1'=4,'frames_2'=2,'heads'=16] {'heads'}, dimensions={0} | all-to-all | bytes 262144 | tf_op jit(solution)/shard_map/all_to_all | solution.py:18
  143.1 19.1 %all_to_all.44 = bf16[16,16,256]{2,1,0:T(8,128)(2,1)S(1)} all-to-all(bf16[16,16,256]{2,1,0:T(8,128)(2,1)S(1)} %broadcast_in_dim.10), channel_id=1, replica_groups=mesh['frames_0'=4,'frames_1'=4,'frames_2'=2,'heads'=16] {'heads'}, dimensions={0} | all-to-all | bytes 262144 | tf_op jit(solution)/shard_map/all_to_all | solution.py:18
  162.5 0.1 copy.92
  162.7 0.3 convolution_convert_fusion
  163.0 0.3 convolution_convert_fusion.1
  163.4 22.0 %all_to_all.45 = bf16[32,8,2176]{2,1,0:T(8,128)(2,1)S(1)} all-to-all(bf16[32,8,2176]{2,1,0:T(8,128)(2,1)S(1)} %fusion.6), channel_id=1, replica_groups=mesh['frames_0'=4,'frames_1'=4,'frames_2'=2,'heads'=16] {'frames_0','fra..., dimensions={0} | all-to-all | bytes 2228224 | tf_op jit(solution)/shard_map/all_to_all | solution.py:18
  185.4 0.2 convert_reduce_fusion
  185.5 0.2 fusion.24
  185.9 15.0 %all_to_all.46 = bf16[32,8,1024]{2,1,0:T(8,128)(2,1)S(1)} all-to-all(bf16[32,8,1024]{2,1,0:T(8,128)(2,1)S(1)} %broadcast_in_dim.11), channel_id=1, replica_groups=mesh['frames_0'=4,'frames_1'=4,'frames_2'=2,'heads'=16] {'frames_0','fra..., dimensions={0} | all-to-all | bytes 1048576 | tf_op jit(solution)/shard_map/all_to_all | solution.py:18
  200.9 0.3 convolution_convert_fusion.4
  201.2 17.9 %all_to_all.47 = bf16[16,16,256]{2,1,0:T(8,128)(2,1)S(1)} all-to-all(bf16[16,16,256]{2,1,0:T(8,128)(2,1)S(1)} %bitcast.86), channel_id=1, replica_groups=mesh['frames_0'=4,'frames_1'=4,'frames_2'=2,'heads'=16] {'heads'}, dimensions={0} | all-to-all | bytes 262144 | tf_op jit(solution)/shard_map/all_to_all | solution.py:18
  219.1 0.6 add_convert_fusion
  (49 shorter events, 1.3 us)
Async XLA Ops:
  6.5 80.2 %copy-start = (bf16[1152,256]{1,0:T(8,128)(2,1)S(1)}, bf16[1152,256]{1,0:T(8,128)(2,1)}, u32[]{:S(2)}) copy-start(bf16[1152,256]{1,0:T(8,128)(2,1)} %param.13) | copy-start | bytes 1769476
  6.5 80.2 %all-gather.2.cloned.1.call-start = ((), (), s32[]{:S(2)}) async-start(), calls=%async_computation.8 | async-start | bytes 2506752 | tf_op jit(solution)/shard_map/all_gather | solution.py:73
  89.3 1.7 copy-start.6
  89.3 1.8 copy-start.7
  91.9 28.8 %copy-start.4 = (bf16[256,256]{1,0:T(8,128)(2,1)S(1)}, bf16[256,256]{1,0:T(8,128)(2,1)}, u32[]{:S(2)}) copy-start(bf16[256,256]{1,0:T(8,128)(2,1)} %param.15) | copy-start | bytes 393220
  92.5 70.1 %copy-start.5 = (f32[256]{0:T(256)S(1)}, f32[256]{0:T(256)}, u32[]{:S(2)}) copy-start(f32[256]{0:T(256)} %param.16) | copy-start | bytes 3076
  92.5 70.2 %copy-start.1 = (bf16[256,1024]{1,0:T(8,128)(2,1)S(1)}, bf16[256,1024]{1,0:T(8,128)(2,1)}, u32[]{:S(2)}) copy-start(bf16[256,1024]{1,0:T(8,128)(2,1)} %param.18) | copy-start | bytes 1572868
  93.1 69.9 %copy-start.2 = (bf16[256,1024]{1,0:T(8,128)(2,1)S(1)}, bf16[256,1024]{1,0:T(8,128)(2,1)}, u32[]{:S(2)}) copy-start(bf16[256,1024]{1,0:T(8,128)(2,1)} %param.17) | copy-start | bytes 1572868
  163.4 37.5 %copy-start.3 = (bf16[1024,256]{1,0:T(8,128)(2,1)S(1)}, bf16[1024,256]{1,0:T(8,128)(2,1)}, u32[]{:S(2)}) copy-start(bf16[1024,256]{1,0:T(8,128)(2,1)} %param.19) | copy-start | bytes 1572868
Sparse Core Ops, SparseCore 0:
  9.4 77.2 all-gather.1

commit v2 on v1

--- a/solution.py
+++ b/solution.py
@@ -12,6 +12,7 @@
 
 
 norm_eps = 1e-06
+SCALE_STEPS = (64, 32, 16, 8, 4, 2)
 
 
 def exchange(blocks, axis):
@@ -52,7 +53,7 @@
     share = rows // peers
     terms = jnp.stack(split_terms(local_max, 3) + split_terms(total, 3), axis=-1)
     stats = terms.reshape(peers, share * heads * 6)
-    stats = jnp.pad(stats, ((0, 0), (0, -stats.shape[1] % HDIM))).reshape(peers, -1, HDIM)
+    stats = jnp.pad(stats, ((0, 0), (0, -stats.shape[1] % (2 * HDIM)))).reshape(peers, -1, HDIM)
     body = mixed.astype(BF16).reshape(peers, share * heads, HDIM)
     arrived = exchange(jnp.concatenate([body, stats], axis=1), FRAMES)
     body = arrived[:, : share * heads].reshape(peers, share, heads, HDIM).astype(F32)
@@ -66,13 +67,36 @@
     return (mixed / total[..., None]).reshape(share, heads * HDIM).astype(BF16)
 
 
+def gathered_features(frames):
+    block = frames.astype(F32)
+    top = jnp.max(jnp.abs(block))
+    scale = jnp.float32(1.0)
+    taken = []
+    for step in SCALE_STEPS:
+        fits = top * 2.0**step <= 60000.0
+        factor = jnp.where(fits, jnp.float32(2.0**step), jnp.float32(1.0))
+        top = top * factor
+        scale = scale * factor
+        taken.append(jnp.where(fits, jnp.float32(1.0), jnp.float32(0.0)))
+    taken += [jnp.float32(0.0)] * 2
+    tokens, width = frames.shape
+    flags = jnp.broadcast_to(jnp.stack(taken)[:, None], (len(taken), tokens))
+    sent = jnp.concatenate([block.T * scale, flags], axis=0).astype(jnp.float16)
+    arrived = lax.all_gather(sent, "heads", axis=0).astype(F32)
+    inverse = jnp.ones((arrived.shape[0], 1, 1), F32)
+    for k, step in enumerate(SCALE_STEPS):
+        flag = arrived[:, width + k : width + k + 1, :1]
+        inverse = inverse * jnp.where(flag > 0.5, jnp.float32(2.0**-step), jnp.float32(1.0))
+    return (arrived[:, :width] * inverse).astype(BF16).reshape(-1, tokens)
+
+
 def on_device(frames, latents, w_query, w_key, w_value, w_out, norm_gain, w_gate, w_up, w_down):
     local_query = jnp.dot(latents, w_query, preferred_element_type=F32).astype(BF16)
     queries = collect_rows(local_query, FRAMES)
     width = w_key.shape[1]
-    piece = lax.all_gather(frames, "heads", axis=1, tiled=True)
-    keys = jnp.dot(piece, w_key, preferred_element_type=F32)
-    values = jnp.dot(piece, w_value, preferred_element_type=F32)
+    piece = gathered_features(frames)
+    keys = jnp.einsum("ft,fc->tc", piece, w_key, preferred_element_type=F32)
+    values = jnp.einsum("ft,fc->tc", piece, w_value, preferred_element_type=F32)
     heads_here = width // HDIM
     latent_count = queries.shape[0]
     query_heads = queries.reshape(latent_count, heads_here, HDIM)

time: 227 us -> 199 us (0.88)
  waiting for transfers between devices: 63.9 us -> 0.01 us
  blocking collectives: 138 us -> 176 us
  between operations: 13.7 us -> 1.69 us
  starting transfers between devices: 0.01 us -> 7.32 us
  other arithmetic: 2.38 us -> 6.56 us
    all_gather x1 -> x0, waiting for transfers between devices: 63.2 us -> none  [on_device(): piece = lax.all_gather(frames, 'heads', axis=1, tiled=True)]
    all_gather x0 -> x1, blocking collectives: none -> 52.3 us  [gathered_features(): arrived = lax.all_gather(sent, 'heads', axis=0).astype(F32)]
    all_to_all x8 -> x7, blocking collectives: 138 us -> 123 us  [exchange(): return lax.all_to_all(blocks, axis, split_axis=0, concat_axis=0, tiled=True)]
    all_to_all x0 -> x1, starting transfers between devices: none -> 7.32 us  [exchange(): return lax.all_to_all(blocks, axis, split_axis=0, concat_axis=0, tiled=True)]
  transfers between devices with their start and end apart: 1 -> 1, of which waited for: 1 -> 0; matrix products, arithmetic and copies ran while one was open for 1% -> 3% of each run, Pallas kernels for 0% -> 0%
where the time goes in v2:
time: 199 us
  blocking collectives  176 us (88%)
  starting transfers between devices  7.32 us (4%)
  other arithmetic  6.56 us (3%)
  matrix products  5.18 us (3%)
  local copies, waits for them, and re-layouts  2.22 us (1%)
    all_to_all x7, blocking collectives, exchange(): return lax.all_to_all(blocks, axis, split_axis=0, concat_axis=0, tiled=True)  123 us
    all_gather x1, blocking collectives, gathered_features(): arrived = lax.all_gather(sent, 'heads', axis=0).astype(F32)  52.3 us
    all_to_all x1, starting transfers between devices, exchange(): return lax.all_to_all(blocks, axis, split_axis=0, concat_axis=0, tiled=True)  7.32 us
  transfers between devices with their start and end apart: 1, of which 0 were waited for; matrix products, arithmetic and copies ran while one was open for 3% of the time, Pallas kernels for 0%

profile of v2, /device:TPU:32, one launch (start us, length us, event | category | flops | bytes accessed | tf_op | source)
XLA Modules:
  0.0 198.7 jit_solution(16411511829979539310)
XLA Ops:
  0.0 1.3 convolution_convert_fusion.7
  1.3 0.7 broadcast_in_dim.71
  2.0 7.3 %all-to-all-start = ((bf16[32,8,256]{2,1,0:T(8,128)(2,1)}), bf16[32,8,256]{2,1,0:T(8,128)(2,1)S(1)}, u32[]{:S(2)}, u32[]{:S(2)}) async-start(bf16[32,8,256]{2,1,0:T(8,128)(2,1)} %broadcast_in_dim.71), calls=%async_computation | async-start | bytes 262144 | tf_op jit(solution)/shard_map/all_to_all | solution.py:19
  9.3 1.5 fusion.12
  12.2 0.9 fusion.15
  13.5 52.3 %all-gather.1 = f16[16,80,1024]{2,1,0:T(8,128)(2,1)S(1)} all-gather(f16[1,80,1024]{2,1,0:T(8,128)(2,1)S(1)} %pad_maximum_fusion.1), channel_id=1, replica_groups=mesh['frames_0'=4,'frames_1'=4,'frames_2'=2,'heads'=16] {'heads'}, dimensions={0}, use_global_device_ids=true | all-gather | bytes 2785280 | tf_op jit(solution)/shard_map/all_gather | solution.py:85
  65.7 0.6 convert_element_type.199
  66.4 0.2 fusion.30
  66.6 0.7 fusion
  67.4 0.9 convolution_convert_fusion.2
  68.3 0.2 copy-done.6
  68.4 0.9 convolution_convert_fusion.3
  69.4 0.5 bitcast_reduce_fusion
  69.9 0.4 fusion.3
  70.3 0.5 fusion.5
  71.0 0.2 copy.78
  71.2 0.2 reshape.222
  71.4 15.5 %all_to_all.40 = bf16[32,18,128]{2,1,0:T(8,128)(2,1)S(1)} all-to-all(bf16[32,18,128]{2,1,0:T(8,128)(2,1)S(1)} %pad_maximum_fusion), channel_id=1, replica_groups=mesh['frames_0'=4,'frames_1'=4,'frames_2'=2,'heads'=16] {'frames_0','fra..., dimensions={0} | all-to-all | bytes 294912 | tf_op jit(solution)/shard_map/all_to_all | solution.py:19
  87.3 0.2 fusion.29
  87.9 11.4 %all_to_all.41 = bf16[32,8,256]{2,1,0:T(8,128)(2,1)S(1)} all-to-all(bf16[32,8,256]{2,1,0:T(8,128)(2,1)S(1)} %broadcast_in_dim.72), channel_id=1, replica_groups=mesh['frames_0'=4,'frames_1'=4,'frames_2'=2,'heads'=16] {'frames_0','fra..., dimensions={0} | all-to-all | bytes 262144 | tf_op jit(solution)/shard_map/all_to_all | solution.py:19
  99.3 0.2 convolution_convert_fusion.5
  99.5 22.5 %all_to_all.42 = bf16[16,16,256]{2,1,0:T(8,128)(2,1)S(1)} all-to-all(bf16[16,16,256]{2,1,0:T(8,128)(2,1)S(1)} %bitcast.93), channel_id=1, replica_groups=mesh['frames_0'=4,'frames_1'=4,'frames_2'=2,'heads'=16] {'heads'}, dimensions={0} | all-to-all | bytes 262144 | tf_op jit(solution)/shard_map/all_to_all | solution.py:19
  122.1 19.1 %all_to_all.43 = bf16[16,16,256]{2,1,0:T(8,128)(2,1)S(1)} all-to-all(bf16[16,16,256]{2,1,0:T(8,128)(2,1)S(1)} %broadcast_in_dim.73), channel_id=1, replica_groups=mesh['frames_0'=4,'frames_1'=4,'frames_2'=2,'heads'=16] {'heads'}, dimensions={0} | all-to-all | bytes 262144 | tf_op jit(solution)/shard_map/all_to_all | solution.py:19
  141.3 0.3 convolution_convert_fusion
  141.6 0.3 convolution_convert_fusion.1
  142.4 22.0 %all_to_all.44 = bf16[32,8,2176]{2,1,0:T(8,128)(2,1)S(1)} all-to-all(bf16[32,8,2176]{2,1,0:T(8,128)(2,1)S(1)} %fusion.7), channel_id=1, replica_groups=mesh['frames_0'=4,'frames_1'=4,'frames_2'=2,'heads'=16] {'frames_0','fra..., dimensions={0} | all-to-all | bytes 2228224 | tf_op jit(solution)/shard_map/all_to_all | solution.py:19
  164.4 0.2 convert_reduce_fusion
  164.5 0.2 fusion.34
  164.9 15.0 %all_to_all.45 = bf16[32,8,1024]{2,1,0:T(8,128)(2,1)S(1)} all-to-all(bf16[32,8,1024]{2,1,0:T(8,128)(2,1)S(1)} %broadcast_in_dim.74), channel_id=1, replica_groups=mesh['frames_0'=4,'frames_1'=4,'frames_2'=2,'heads'=16] {'frames_0','fra..., dimensions={0} | all-to-all | bytes 1048576 | tf_op jit(solution)/shard_map/all_to_all | solution.py:19
  179.9 0.3 convolution_convert_fusion.4
  180.2 17.9 %all_to_all.46 = bf16[16,16,256]{2,1,0:T(8,128)(2,1)S(1)} all-to-all(bf16[16,16,256]{2,1,0:T(8,128)(2,1)S(1)} %bitcast.94), channel_id=1, replica_groups=mesh['frames_0'=4,'frames_1'=4,'frames_2'=2,'heads'=16] {'heads'}, dimensions={0} | all-to-all | bytes 262144 | tf_op jit(solution)/shard_map/all_to_all | solution.py:19
  198.1 0.6 add_convert_fusion
  (56 shorter events, 2.0 us)
Async XLA Ops:
  0.0 67.3 %copy-start = (bf16[1152,256]{1,0:T(8,128)(2,1)S(1)}, bf16[1152,256]{1,0:T(8,128)(2,1)}, u32[]{:S(2)}) copy-start(bf16[1152,256]{1,0:T(8,128)(2,1)} %param.13) | copy-start | bytes 1769476
  2.0 67.3 %all-to-all-start = ((bf16[32,8,256]{2,1,0:T(8,128)(2,1)}), bf16[32,8,256]{2,1,0:T(8,128)(2,1)S(1)}, u32[]{:S(2)}, u32[]{:S(2)}) async-start(bf16[32,8,256]{2,1,0:T(8,128)(2,1)} %broadcast_in_dim.71), calls=%async_computation | async-start | bytes 262144 | tf_op jit(solution)/shard_map/all_to_all | solution.py:19
  67.4 1.1 copy-start.6
  70.2 29.1 %copy-start.4 = (bf16[256,256]{1,0:T(8,128)(2,1)S(1)}, bf16[256,256]{1,0:T(8,128)(2,1)}, u32[]{:S(2)}) copy-start(bf16[256,256]{1,0:T(8,128)(2,1)} %param.15) | copy-start | bytes 393220
  70.8 70.5 %copy-start.5 = (f32[256]{0:T(256)S(1)}, f32[256]{0:T(256)}, u32[]{:S(2)}) copy-start(f32[256]{0:T(256)} %param.16) | copy-start | bytes 3076
  70.8 70.5 %copy-start.1 = (bf16[256,1024]{1,0:T(8,128)(2,1)S(1)}, bf16[256,1024]{1,0:T(8,128)(2,1)}, u32[]{:S(2)}) copy-start(bf16[256,1024]{1,0:T(8,128)(2,1)} %param.18) | copy-start | bytes 1572868
  71.4 70.2 %copy-start.2 = (bf16[256,1024]{1,0:T(8,128)(2,1)S(1)}, bf16[256,1024]{1,0:T(8,128)(2,1)}, u32[]{:S(2)}) copy-start(bf16[256,1024]{1,0:T(8,128)(2,1)} %param.17) | copy-start | bytes 1572868
  142.4 37.5 %copy-start.3 = (bf16[1024,256]{1,0:T(8,128)(2,1)S(1)}, bf16[1024,256]{1,0:T(8,128)(2,1)}, u32[]{:S(2)}) copy-start(bf16[1024,256]{1,0:T(8,128)(2,1)} %param.19) | copy-start | bytes 1572868

commit v3 on v1

--- a/solution.py
+++ b/solution.py
@@ -7,11 +7,14 @@
 HDIM = 128
 D = 8192
 FRAMES = ("frames_0", "frames_1", "frames_2")
+CHIPS = ("frames_0", "frames_1")
+CORE = "frames_2"
 BF16 = jnp.bfloat16
 F32 = jnp.float32
 
 
 norm_eps = 1e-06
+LANES = 128
 
 
 def exchange(blocks, axis):
@@ -52,7 +55,7 @@
     share = rows // peers
     terms = jnp.stack(split_terms(local_max, 3) + split_terms(total, 3), axis=-1)
     stats = terms.reshape(peers, share * heads * 6)
-    stats = jnp.pad(stats, ((0, 0), (0, -stats.shape[1] % HDIM))).reshape(peers, -1, HDIM)
+    stats = jnp.pad(stats, ((0, 0), (0, -stats.shape[1] % (2 * HDIM)))).reshape(peers, -1, HDIM)
     body = mixed.astype(BF16).reshape(peers, share * heads, HDIM)
     arrived = exchange(jnp.concatenate([body, stats], axis=1), FRAMES)
     body = arrived[:, : share * heads].reshape(peers, share, heads, HDIM).astype(F32)
@@ -66,13 +69,34 @@
     return (mixed / total[..., None]).reshape(share, heads * HDIM).astype(BF16)
 
 
+def power_near(value):
+    return lax.reduce_precision(value, 8, 0)
+
+
+def gathered_features(frames):
+    tokens, width = frames.shape
+    top = jnp.maximum(jnp.max(jnp.abs(frames)).astype(F32), 2.0**-108)
+    exponent = jnp.round(jnp.log2(top))
+    scale = power_near(jnp.exp2(14.0 - exponent))
+    groups = tokens // LANES
+    block = frames.astype(F32).T.reshape(width, groups, LANES).transpose(1, 0, 2) * scale
+    tail = jnp.broadcast_to(exponent, (8, LANES))
+    sent = jnp.concatenate([block.reshape(-1, LANES), tail], axis=0).astype(jnp.float16)
+    arrived = lax.all_gather(sent.reshape(-1, 8, LANES), "heads", axis=0)
+    peers = arrived.shape[0]
+    inverse = power_near(jnp.exp2(arrived[:, width, :1, :1].astype(F32) - 14.0))
+    features = arrived[:, :width].reshape(peers, groups, width, LANES).astype(F32)
+    features = (features * inverse[:, None]).astype(BF16)
+    return features.transpose(0, 2, 1, 3).reshape(peers * width, tokens)
+
+
 def on_device(frames, latents, w_query, w_key, w_value, w_out, norm_gain, w_gate, w_up, w_down):
     local_query = jnp.dot(latents, w_query, preferred_element_type=F32).astype(BF16)
     queries = collect_rows(local_query, FRAMES)
     width = w_key.shape[1]
-    piece = lax.all_gather(frames, "heads", axis=1, tiled=True)
-    keys = jnp.dot(piece, w_key, preferred_element_type=F32)
-    values = jnp.dot(piece, w_value, preferred_element_type=F32)
+    piece = gathered_features(frames)
+    keys = jnp.einsum("ft,fc->tc", piece, w_key, preferred_element_type=F32)
+    values = jnp.einsum("ft,fc->tc", piece, w_value, preferred_element_type=F32)
     heads_here = width // HDIM
     latent_count = queries.shape[0]
     query_heads = queries.reshape(latent_count, heads_here, HDIM)
@@ -91,18 +115,35 @@
     ).astype(BF16)
     latent_full = collect_rows(latent_state, "heads")
     full_float = latent_full.astype(F32)
-    square_part = jnp.sum(full_float * full_float, axis=1)
     normed = (full_float * norm_gain[None, :]).astype(BF16)
-    gate_part = jnp.dot(normed, w_gate, preferred_element_type=F32).astype(BF16)
-    up_part = jnp.dot(normed, w_up, preferred_element_type=F32).astype(BF16)
-    square_terms = jnp.stack(split_terms(square_part, 2), axis=1)
-    square_terms = jnp.pad(square_terms, ((0, 0), (0, 126)))
-    peers = lax.axis_size(FRAMES)
-    packed = jnp.concatenate([gate_part, up_part, square_terms], axis=1)
-    sums = jnp.sum(exchange(packed.reshape(peers, -1, packed.shape[1]), FRAMES).astype(F32), axis=0)
+    square_part = jnp.sum(full_float * full_float, axis=1, keepdims=True)
     units = w_gate.shape[1]
-    gate_sum, up_sum = sums[:, :units], sums[:, units : 2 * units]
-    squares = sums[:, 2 * units : 2 * units + 1] + sums[:, 2 * units + 1 : 2 * units + 2]
+    core = lax.axis_index(CORE)
+    share = latent_count // lax.axis_size(FRAMES)
+
+    def rows_of(array, owner):
+        blocks = array.reshape(lax.axis_size(CHIPS), 2, share, array.shape[1])
+        return lax.dynamic_index_in_dim(blocks, owner, 1, keepdims=False).reshape(-1, array.shape[1])
+
+    def partial_sums(owner):
+        rows = rows_of(normed, owner)
+        gate = jnp.dot(rows, w_gate, preferred_element_type=F32)
+        up = jnp.dot(rows, w_up, preferred_element_type=F32)
+        return gate, up, rows_of(square_part, owner)
+
+    def packed(gate, up, squares):
+        terms = jnp.pad(jnp.concatenate(split_terms(squares, 2), axis=1), ((0, 0), (0, 126)))
+        return jnp.concatenate([gate.astype(BF16), up.astype(BF16), terms], axis=1)
+
+    def unpacked(sums):
+        squares = sums[:, 2 * units : 2 * units + 1] + sums[:, 2 * units + 1 : 2 * units + 2]
+        return sums[:, :units], sums[:, units : 2 * units], squares
+
+    handed = lax.ppermute(packed(*partial_sums(1 - core)), CORE, [(0, 1), (1, 0)])
+    theirs = unpacked(handed.astype(F32))
+    blocks = packed(*[a + b for a, b in zip(partial_sums(core), theirs)])
+    blocks = exchange(blocks.reshape(-1, share, blocks.shape[1]), CHIPS)
+    gate_sum, up_sum, squares = unpacked(jnp.sum(blocks.astype(F32), axis=0))
     scale_rows = lax.rsqrt(squares / D + norm_eps)
     hidden = (jax.nn.silu(gate_sum * scale_rows) * (up_sum * scale_rows)).astype(BF16)
     hidden_full = collect_rows(hidden, FRAMES)

time: 227 us -> 197 us (0.87)
  waiting for transfers between devices: 63.9 us -> 16.2 us
  starting transfers between devices: 0.01 us -> 14.2 us
  between operations: 13.7 us -> 1.68 us
  blocking collectives: 138 us -> 147 us
  other arithmetic: 2.38 us -> 6.89 us
    all_gather x1 -> x0, waiting for transfers between devices: 63.2 us -> none  [on_device(): piece = lax.all_gather(frames, 'heads', axis=1, tiled=True)]
    all_gather x0 -> x1, blocking collectives: none -> 50.6 us  [gathered_features(): arrived = lax.all_gather(sent.reshape(-1, 8, LANES), 'heads', axis=0)]
    all_to_all x8 -> x6, blocking collectives: 138 us -> 96.9 us  [exchange(): return lax.all_to_all(blocks, axis, split_axis=0, concat_axis=0, tiled=True)]
    all_to_all x0 -> x2, waiting for transfers between devices: none -> 14.5 us  [exchange(): return lax.all_to_all(blocks, axis, split_axis=0, concat_axis=0, tiled=True)]
    all_to_all x0 -> x2, starting transfers between devices: none -> 12.2 us  [exchange(): return lax.all_to_all(blocks, axis, split_axis=0, concat_axis=0, tiled=True)]
  transfers between devices with their start and end apart: 1 -> 3, of which waited for: 1 -> 2; matrix products, arithmetic and copies ran while one was open for 1% -> 4% of each run, Pallas kernels for 0% -> 0%
where the time goes in v3:
time: 197 us; the launch traced here: 196 us
  blocking collectives  147 us (75%)
  waiting for transfers between devices  16.2 us (8%)
  starting transfers between devices  14.2 us (7%)
  other arithmetic  6.89 us (3%)
  matrix products  5.96 us (3%)
  local copies, waits for them, and re-layouts  3.96 us (2%)
    all_to_all x6, blocking collectives, exchange(): return lax.all_to_all(blocks, axis, split_axis=0, concat_axis=0, tiled=True)  96.9 us
    all_gather x1, blocking collectives, gathered_features(): arrived = lax.all_gather(sent.reshape(-1, 8, LANES), 'heads', axis=0)  50.6 us
    all_to_all x2, waiting for transfers between devices, exchange(): return lax.all_to_all(blocks, axis, split_axis=0, concat_axis=0, tiled=True)  14.5 us
    all_to_all x2, starting transfers between devices, exchange(): return lax.all_to_all(blocks, axis, split_axis=0, concat_axis=0, tiled=True)  12.2 us
  transfers between devices with their start and end apart: 3, of which 2 were waited for; matrix products, arithmetic and copies ran while one was open for 4% of the time, Pallas kernels for 0%

profile of v3, /device:TPU:32, one launch (start us, length us, event | category | flops | bytes accessed | tf_op | source)
XLA Modules:
  0.0 196.3 jit_solution(5124199700110263965)
XLA Ops:
  0.0 1.3 convolution_convert_fusion.5
  1.3 0.7 broadcast_in_dim.8
  2.0 7.3 %all-to-all-start = ((bf16[32,8,256]{2,1,0:T(8,128)(2,1)}), bf16[32,8,256]{2,1,0:T(8,128)(2,1)S(1)}, u32[]{:S(2)}, u32[]{:S(2)}) async-start(bf16[32,8,256]{2,1,0:T(8,128)(2,1)} %broadcast_in_dim.8), calls=%async_computation | async-start | bytes 262144 | tf_op jit(solution)/shard_map/all_to_all | solution.py:21
  9.3 1.5 abs_reduce_fusion
  12.1 1.6 fusion.26
  13.9 50.6 %all-gather.1 = f16[16,73,8,128]{3,2,1,0:T(8,128)(2,1)S(1)} all-gather(f16[1,73,8,128]{3,2,1,0:T(8,128)(2,1)S(1)} %pad_bitcast_fusion), channel_id=1, replica_groups=mesh['frames_0'=4,'frames_1'=4,'frames_2'=2,'heads'=16] {'heads'}, dimensions={0}, use_global_device_ids=true | all-gather | bytes 2541568 | tf_op jit(solution)/shard_map/all_gather | solution.py:85
  64.5 0.6 slice.76
  65.2 0.3 bitcast_convert_fusion
  65.5 1.0 fusion
  66.6 0.9 fusion.13
  67.6 0.9 fusion.10
  68.6 0.5 bitcast_reduce_fusion
  69.1 0.4 fusion.8
  69.4 0.5 fusion.16
  70.6 15.2 %all_to_all.40 = bf16[32,18,128]{2,1,0:T(8,128)(2,1)S(1)} all-to-all(bf16[32,18,128]{2,1,0:T(8,128)(2,1)S(1)} %pad_maximum_fusion.2), channel_id=1, replica_groups=mesh['frames_0'=4,'frames_1'=4,'frames_2'=2,'heads'=16] {'frames_0','fra..., dimensions={0} | all-to-all | bytes 294912 | tf_op jit(solution)/shard_map/all_to_all | solution.py:21
  86.8 11.4 %all_to_all.41 = bf16[32,8,256]{2,1,0:T(8,128)(2,1)S(1)} all-to-all(bf16[32,8,256]{2,1,0:T(8,128)(2,1)S(1)} %broadcast_in_dim.9), channel_id=1, replica_groups=mesh['frames_0'=4,'frames_1'=4,'frames_2'=2,'heads'=16] {'frames_0','fra..., dimensions={0} | all-to-all | bytes 262144 | tf_op jit(solution)/shard_map/all_to_all | solution.py:21
  98.4 22.1 %all_to_all.42 = bf16[16,16,256]{2,1,0:T(8,128)(2,1)S(1)} all-to-all(bf16[16,16,256]{2,1,0:T(8,128)(2,1)S(1)} %bitcast.135), channel_id=1, replica_groups=mesh['frames_0'=4,'frames_1'=4,'frames_2'=2,'heads'=16] {'heads'}, dimensions={0} | all-to-all | bytes 262144 | tf_op jit(solution)/shard_map/all_to_all | solution.py:21
  120.5 0.6 broadcast_in_dim.10
  121.1 4.9 %all-to-all-start.4 = ((bf16[16,16,256]{2,1,0:T(8,128)(2,1)}), bf16[16,16,256]{2,1,0:T(8,128)(2,1)S(1)}, u32[]{:S(2)}, u32[]{:S(2)}) async-start(bf16[16,16,256]{2,1,0:T(8,128)(2,1)} %broadcast_in_dim.10), calls=%async_computation.4 | async-start | bytes 262144 | tf_op jit(solution)/shard_map/all_to_all | solution.py:21
  126.0 14.5 %all-to-all-done.4 = bf16[16,16,256]{2,1,0:T(8,128)(2,1)S(1)} async-done(((bf16[16,16,256]{2,1,0:T(8,128)(2,1)}), bf16[16,16,256]{2,1,0:T(8,128)(2,1)S(1)}, u32[]{:S(2)}, u32[]{:S(2)}) %all-to-all-start.4) | async-done | bytes 131104 | tf_op jit(solution)/shard_map/all_to_all | solution.py:21
  140.9 0.3 convolution_convert_fusion
  141.3 0.3 convolution_convert_fusion.1
  141.7 1.9 collective-permute-start
  143.8 1.8 collective-permute-done
  145.6 0.3 fusion.20
  146.0 0.4 fusion.21
  146.4 0.3 copy.153
  146.7 15.4 %all_to_all.43 = bf16[16,8,2176]{2,1,0:T(8,128)(2,1)S(1)} all-to-all(bf16[16,8,2176]{2,1,0:T(8,128)(2,1)S(1)} %bitcast.132), channel_id=1, replica_groups=mesh['frames_0'=4,'frames_1'=4,'frames_2'=2,'heads'=16] {'frames_0','fra..., dimensions={0} | all-to-all | bytes 1114112 | tf_op jit(solution)/shard_map/all_to_all | solution.py:21
  162.6 14.9 %all_to_all.44 = bf16[32,8,1024]{2,1,0:T(8,128)(2,1)S(1)} all-to-all(bf16[32,8,1024]{2,1,0:T(8,128)(2,1)S(1)} %broadcast_in_dim.11), channel_id=1, replica_groups=mesh['frames_0'=4,'frames_1'=4,'frames_2'=2,'heads'=16] {'frames_0','fra..., dimensions={0} | all-to-all | bytes 1048576 | tf_op jit(solution)/shard_map/all_to_all | solution.py:21
  177.5 0.3 convolution_convert_fusion.2
  177.8 17.9 %all_to_all.45 = bf16[16,16,256]{2,1,0:T(8,128)(2,1)S(1)} all-to-all(bf16[16,16,256]{2,1,0:T(8,128)(2,1)S(1)} %bitcast.136), channel_id=1, replica_groups=mesh['frames_0'=4,'frames_1'=4,'frames_2'=2,'heads'=16] {'heads'}, dimensions={0} | all-to-all | bytes 262144 | tf_op jit(solution)/shard_map/all_to_all | solution.py:21
  195.7 0.6 add_convert_fusion
  (72 shorter events, 3.4 us)
Async XLA Ops:
  0.0 66.5 %copy-start = (bf16[1152,256]{1,0:T(8,128)(2,1)S(1)}, bf16[1152,256]{1,0:T(8,128)(2,1)}, u32[]{:S(2)}) copy-start(bf16[1152,256]{1,0:T(8,128)(2,1)} %param.13) | copy-start | bytes 1769476
  2.0 66.5 %all-to-all-start = ((bf16[32,8,256]{2,1,0:T(8,128)(2,1)}), bf16[32,8,256]{2,1,0:T(8,128)(2,1)S(1)}, u32[]{:S(2)}, u32[]{:S(2)}) async-start(bf16[32,8,256]{2,1,0:T(8,128)(2,1)} %broadcast_in_dim.8), calls=%async_computation | async-start | bytes 262144 | tf_op jit(solution)/shard_map/all_to_all | solution.py:21
  66.5 1.1 copy-start.6
  69.4 28.8 %copy-start.4 = (bf16[256,256]{1,0:T(8,128)(2,1)S(1)}, bf16[256,256]{1,0:T(8,128)(2,1)}, u32[]{:S(2)}) copy-start(bf16[256,256]{1,0:T(8,128)(2,1)} %param.15) | copy-start | bytes 393220
  70.0 70.9 %copy-start.5 = (f32[256]{0:T(256)S(1)}, f32[256]{0:T(256)}, u32[]{:S(2)}) copy-start(f32[256]{0:T(256)} %param.16) | copy-start | bytes 3076
  70.0 71.0 %copy-start.1 = (bf16[256,1024]{1,0:T(8,128)(2,1)S(1)}, bf16[256,1024]{1,0:T(8,128)(2,1)}, u32[]{:S(2)}) copy-start(bf16[256,1024]{1,0:T(8,128)(2,1)} %param.18) | copy-start | bytes 1572868
  70.5 70.7 %copy-start.2 = (bf16[256,1024]{1,0:T(8,128)(2,1)S(1)}, bf16[256,1024]{1,0:T(8,128)(2,1)}, u32[]{:S(2)}) copy-start(bf16[256,1024]{1,0:T(8,128)(2,1)} %param.17) | copy-start | bytes 1572868
  121.1 19.4 %all-to-all-start.4 = ((bf16[16,16,256]{2,1,0:T(8,128)(2,1)}), bf16[16,16,256]{2,1,0:T(8,128)(2,1)S(1)}, u32[]{:S(2)}, u32[]{:S(2)}) async-start(bf16[16,16,256]{2,1,0:T(8,128)(2,1)} %broadcast_in_dim.10), calls=%async_computation.4 | async-start | bytes 262144 | tf_op jit(solution)/shard_map/all_to_all | solution.py:21
  141.7 3.9 %collective-permute-start = (bf16[128,2176]{0,1:T(8,128)(2,1)S(1)}, bf16[128,2176]{0,1:T(8,128)(2,1)S(1)}, u32[]{:S(2)}, u32[]{:S(2)}) collective-permute-start(bf16[128,2176]{0,1:T(8,128)(2,1)S(1)} %pad_maximum_fusion), channel_id=1, source_target_pairs={{0,16},{16,0},{1,17},{17,1},{2,18},{18,2},{3,19},{19,3},{4,20},{20... | collective-permute-start | bytes 1671176 | tf_op jit(solution)/shard_map/ppermute | solution.py:142
  146.4 31.1 %copy-start.3 = (bf16[1024,256]{1,0:T(8,128)(2,1)S(1)}, bf16[1024,256]{1,0:T(8,128)(2,1)}, u32[]{:S(2)}) copy-start(bf16[1024,256]{1,0:T(8,128)(2,1)} %param.19) | copy-start | bytes 1572868

commit v4 on v3

--- a/solution.py
+++ b/solution.py
@@ -75,13 +75,16 @@
 
 def gathered_features(frames):
     tokens, width = frames.shape
-    top = jnp.maximum(jnp.max(jnp.abs(frames)).astype(F32), 2.0**-108)
-    exponent = jnp.round(jnp.log2(top))
+    groups = tokens // LANES
+    block = lax.optimization_barrier(frames.astype(F32).T)
+    top = jnp.max(jnp.max(jnp.abs(block).reshape(-1, 8, tokens), axis=0).reshape(8, groups, LANES), axis=1)
+    top = lax.optimization_barrier(jnp.max(top, keepdims=True))
+    top = jnp.maximum(jnp.broadcast_to(top, (8, LANES)), 2.0**-108)
+    exponent = lax.optimization_barrier(jnp.round(jnp.log2(top)))
     scale = power_near(jnp.exp2(14.0 - exponent))
-    groups = tokens // LANES
-    block = frames.astype(F32).T.reshape(width, groups, LANES).transpose(1, 0, 2) * scale
-    tail = jnp.broadcast_to(exponent, (8, LANES))
-    sent = jnp.concatenate([block.reshape(-1, LANES), tail], axis=0).astype(jnp.float16)
+    block = (block.reshape(-1, 8, groups, LANES) * scale[:, None]).astype(jnp.float16)
+    block = block.transpose(2, 0, 1, 3).reshape(-1, LANES)
+    sent = jnp.concatenate([block, exponent.astype(jnp.float16)], axis=0)
     arrived = lax.all_gather(sent.reshape(-1, 8, LANES), "heads", axis=0)
     peers = arrived.shape[0]
     inverse = power_near(jnp.exp2(arrived[:, width, :1, :1].astype(F32) - 14.0))
@@ -91,6 +94,8 @@
 
 
 def on_device(frames, latents, w_query, w_key, w_value, w_out, norm_gain, w_gate, w_up, w_down):
+    core = lax.convert_element_type(lax.axis_index(CORE), jnp.uint32)
+    core, other, latents = lax.optimization_barrier((core, jnp.uint32(1) - core, latents))
     local_query = jnp.dot(latents, w_query, preferred_element_type=F32).astype(BF16)
     queries = collect_rows(local_query, FRAMES)
     width = w_key.shape[1]
@@ -118,7 +123,6 @@
     normed = (full_float * norm_gain[None, :]).astype(BF16)
     square_part = jnp.sum(full_float * full_float, axis=1, keepdims=True)
     units = w_gate.shape[1]
-    core = lax.axis_index(CORE)
     share = latent_count // lax.axis_size(FRAMES)
 
     def rows_of(array, owner):
@@ -139,7 +143,7 @@
         squares = sums[:, 2 * units : 2 * units + 1] + sums[:, 2 * units + 1 : 2 * units + 2]
         return sums[:, :units], sums[:, units : 2 * units], squares
 
-    handed = lax.ppermute(packed(*partial_sums(1 - core)), CORE, [(0, 1), (1, 0)])
+    handed = lax.ppermute(packed(*partial_sums(other)), CORE, [(0, 1), (1, 0)])
     theirs = unpacked(handed.astype(F32))
     blocks = packed(*[a + b for a, b in zip(partial_sums(core), theirs)])
     blocks = exchange(blocks.reshape(-1, share, blocks.shape[1]), CHIPS)

time: 197 us -> 194 us (0.985)
  blocking collectives: 147 us -> 167 us
  waiting for transfers between devices: 16.2 us -> 1.76 us
  starting transfers between devices: 14.2 us -> 9.24 us
    all_to_all x6 -> x7, blocking collectives: 96.9 us -> 116 us  [exchange(): return lax.all_to_all(blocks, axis, split_axis=0, concat_axis=0, tiled=True)]
    all_to_all x2 -> x1, waiting for transfers between devices: 14.5 us -> 0.01 us  [exchange(): return lax.all_to_all(blocks, axis, split_axis=0, concat_axis=0, tiled=True)]
    all_to_all x2 -> x1, starting transfers between devices: 12.2 us -> 7.32 us  [exchange(): return lax.all_to_all(blocks, axis, split_axis=0, concat_axis=0, tiled=True)]
  transfers between devices with their start and end apart: 3 -> 2, of which waited for: 2 -> 1; matrix products, arithmetic and copies ran while one was open for 4% -> 3% of each run, Pallas kernels for 0% -> 0%
where the time goes in v4:
time: 194 us; the launch traced here: 193 us
  blocking collectives  167 us (86%)
  starting transfers between devices  9.24 us (5%)
  matrix products  5.96 us (3%)
  other arithmetic  5.43 us (3%)
  local copies, waits for them, and re-layouts  3.24 us (2%)
    all_to_all x7, blocking collectives, exchange(): return lax.all_to_all(blocks, axis, split_axis=0, concat_axis=0, tiled=True)  116 us
    all_gather x1, blocking collectives, gathered_features(): arrived = lax.all_gather(sent.reshape(-1, 8, LANES), 'heads', axis=0)  50.6 us
    all_to_all x1, starting transfers between devices, exchange(): return lax.all_to_all(blocks, axis, split_axis=0, concat_axis=0, tiled=True)  7.32 us
  transfers between devices with their start and end apart: 2, of which 1 were waited for; matrix products, arithmetic and copies ran while one was open for 3% of the time, Pallas kernels for 0%

profile of v4, /device:TPU:32, one launch (start us, length us, event | category | flops | bytes accessed | tf_op | source)
XLA Modules:
  0.0 193.4 jit_solution(10576825673704700450)
XLA Ops:
  0.0 1.3 convolution_convert_fusion.5
  1.3 0.7 broadcast_in_dim.11
  2.0 7.3 %all-to-all-start = ((bf16[32,8,256]{2,1,0:T(8,128)(2,1)}), bf16[32,8,256]{2,1,0:T(8,128)(2,1)S(1)}, u32[]{:S(2)}, u32[]{:S(2)}) async-start(bf16[32,8,256]{2,1,0:T(8,128)(2,1)} %broadcast_in_dim.11), calls=%async_computation | async-start | bytes 262144 | tf_op jit(solution)/shard_map/all_to_all | solution.py:21
  9.3 0.9 convert_bitcast_fusion.1
  10.3 0.6 abs_reduce_fusion
  11.8 50.6 %all-gather.1 = f16[16,73,8,128]{3,2,1,0:T(8,128)(2,1)S(1)} all-gather(f16[1,73,8,128]{3,2,1,0:T(8,128)(2,1)S(1)} %maximum_bitcast_fusion), channel_id=1, replica_groups=mesh['frames_0'=4,'frames_1'=4,'frames_2'=2,'heads'=16] {'heads'}, dimensions={0}, use_global_device_ids=true | all-gather | bytes 2541568 | tf_op jit(solution)/shard_map/all_gather | solution.py:88
  62.4 0.6 slice.76
  63.1 0.3 bitcast_convert_fusion
  63.4 1.0 fusion
  64.5 0.9 fusion.13
  65.5 0.9 fusion.10
  66.5 0.5 bitcast_reduce_fusion
  67.0 0.4 fusion.8
  67.3 0.5 fusion.16
  68.5 15.2 %all_to_all.40 = bf16[32,18,128]{2,1,0:T(8,128)(2,1)S(1)} all-to-all(bf16[32,18,128]{2,1,0:T(8,128)(2,1)S(1)} %pad_maximum_fusion.2), channel_id=1, replica_groups=mesh['frames_0'=4,'frames_1'=4,'frames_2'=2,'heads'=16] {'frames_0','fra..., dimensions={0} | all-to-all | bytes 294912 | tf_op jit(solution)/shard_map/all_to_all | solution.py:21
  84.7 11.4 %all_to_all.41 = bf16[32,8,256]{2,1,0:T(8,128)(2,1)S(1)} all-to-all(bf16[32,8,256]{2,1,0:T(8,128)(2,1)S(1)} %broadcast_in_dim.12), channel_id=1, replica_groups=mesh['frames_0'=4,'frames_1'=4,'frames_2'=2,'heads'=16] {'frames_0','fra..., dimensions={0} | all-to-all | bytes 262144 | tf_op jit(solution)/shard_map/all_to_all | solution.py:21
  96.1 0.2 convolution_convert_fusion.3
  96.3 22.1 %all_to_all.42 = bf16[16,16,256]{2,1,0:T(8,128)(2,1)S(1)} all-to-all(bf16[16,16,256]{2,1,0:T(8,128)(2,1)S(1)} %bitcast.143), channel_id=1, replica_groups=mesh['frames_0'=4,'frames_1'=4,'frames_2'=2,'heads'=16] {'heads'}, dimensions={0} | all-to-all | bytes 262144 | tf_op jit(solution)/shard_map/all_to_all | solution.py:21
  118.4 19.2 %all_to_all.43 = bf16[16,16,256]{2,1,0:T(8,128)(2,1)S(1)} all-to-all(bf16[16,16,256]{2,1,0:T(8,128)(2,1)S(1)} %broadcast_in_dim.13), channel_id=1, replica_groups=mesh['frames_0'=4,'frames_1'=4,'frames_2'=2,'heads'=16] {'heads'}, dimensions={0} | all-to-all | bytes 262144 | tf_op jit(solution)/shard_map/all_to_all | solution.py:21
  138.0 0.3 convolution_convert_fusion
  138.3 0.3 convolution_convert_fusion.1
  138.8 1.9 collective-permute-start
  140.9 1.8 collective-permute-done
  142.7 0.3 fusion.20
  143.0 0.4 fusion.21
  143.5 0.3 copy.153
  143.8 15.4 %all_to_all.44 = bf16[16,8,2176]{2,1,0:T(8,128)(2,1)S(1)} all-to-all(bf16[16,8,2176]{2,1,0:T(8,128)(2,1)S(1)} %bitcast.141), channel_id=1, replica_groups=mesh['frames_0'=4,'frames_1'=4,'frames_2'=2,'heads'=16] {'frames_0','fra..., dimensions={0} | all-to-all | bytes 1114112 | tf_op jit(solution)/shard_map/all_to_all | solution.py:21
  159.3 0.2 fusion.60
  159.6 14.9 %all_to_all.45 = bf16[32,8,1024]{2,1,0:T(8,128)(2,1)S(1)} all-to-all(bf16[32,8,1024]{2,1,0:T(8,128)(2,1)S(1)} %broadcast_in_dim.14), channel_id=1, replica_groups=mesh['frames_0'=4,'frames_1'=4,'frames_2'=2,'heads'=16] {'frames_0','fra..., dimensions={0} | all-to-all | bytes 1048576 | tf_op jit(solution)/shard_map/all_to_all | solution.py:21
  174.6 0.3 convolution_convert_fusion.2
  174.9 17.9 %all_to_all.46 = bf16[16,16,256]{2,1,0:T(8,128)(2,1)S(1)} all-to-all(bf16[16,16,256]{2,1,0:T(8,128)(2,1)S(1)} %bitcast.144), channel_id=1, replica_groups=mesh['frames_0'=4,'frames_1'=4,'frames_2'=2,'heads'=16] {'heads'}, dimensions={0} | all-to-all | bytes 262144 | tf_op jit(solution)/shard_map/all_to_all | solution.py:21
  192.8 0.6 add_convert_fusion
  (73 shorter events, 3.1 us)
Async XLA Ops:
  0.0 64.4 %copy-start = (bf16[1152,256]{1,0:T(8,128)(2,1)S(1)}, bf16[1152,256]{1,0:T(8,128)(2,1)}, u32[]{:S(2)}) copy-start(bf16[1152,256]{1,0:T(8,128)(2,1)} %param.13) | copy-start | bytes 1769476
  2.0 64.4 %all-to-all-start = ((bf16[32,8,256]{2,1,0:T(8,128)(2,1)}), bf16[32,8,256]{2,1,0:T(8,128)(2,1)S(1)}, u32[]{:S(2)}, u32[]{:S(2)}) async-start(bf16[32,8,256]{2,1,0:T(8,128)(2,1)} %broadcast_in_dim.11), calls=%async_computation | async-start | bytes 262144 | tf_op jit(solution)/shard_map/all_to_all | solution.py:21
  64.4 1.1 copy-start.6
  67.3 28.8 %copy-start.4 = (bf16[256,256]{1,0:T(8,128)(2,1)S(1)}, bf16[256,256]{1,0:T(8,128)(2,1)}, u32[]{:S(2)}) copy-start(bf16[256,256]{1,0:T(8,128)(2,1)} %param.15) | copy-start | bytes 393220
  67.9 70.1 %copy-start.5 = (f32[256]{0:T(256)S(1)}, f32[256]{0:T(256)}, u32[]{:S(2)}) copy-start(f32[256]{0:T(256)} %param.16) | copy-start | bytes 3076
  67.9 70.1 %copy-start.1 = (bf16[256,1024]{1,0:T(8,128)(2,1)S(1)}, bf16[256,1024]{1,0:T(8,128)(2,1)}, u32[]{:S(2)}) copy-start(bf16[256,1024]{1,0:T(8,128)(2,1)} %param.18) | copy-start | bytes 1572868
  68.4 69.9 %copy-start.2 = (bf16[256,1024]{1,0:T(8,128)(2,1)S(1)}, bf16[256,1024]{1,0:T(8,128)(2,1)}, u32[]{:S(2)}) copy-start(bf16[256,1024]{1,0:T(8,128)(2,1)} %param.17) | copy-start | bytes 1572868
  138.8 3.9 %collective-permute-start = (bf16[128,2176]{0,1:T(8,128)(2,1)S(1)}, bf16[128,2176]{0,1:T(8,128)(2,1)S(1)}, u32[]{:S(2)}, u32[]{:S(2)}) collective-permute-start(bf16[128,2176]{0,1:T(8,128)(2,1)S(1)} %pad_maximum_fusion), channel_id=1, source_target_pairs={{0,16},{16,0},{1,17},{17,1},{2,18},{18,2},{3,19},{19,3},{4,20},{20... | collective-permute-start | bytes 1671176 | tf_op jit(solution)/shard_map/ppermute | solution.py:146
  143.5 31.1 %copy-start.3 = (bf16[1024,256]{1,0:T(8,128)(2,1)S(1)}, bf16[1024,256]{1,0:T(8,128)(2,1)}, u32[]{:S(2)}) copy-start(bf16[1024,256]{1,0:T(8,128)(2,1)} %param.19) | copy-start | bytes 1572868

commit v5 on v4

--- a/solution.py
+++ b/solution.py
@@ -139,15 +139,18 @@
         terms = jnp.pad(jnp.concatenate(split_terms(squares, 2), axis=1), ((0, 0), (0, 126)))
         return jnp.concatenate([gate.astype(BF16), up.astype(BF16), terms], axis=1)
 
-    def unpacked(sums):
-        squares = sums[:, 2 * units : 2 * units + 1] + sums[:, 2 * units + 1 : 2 * units + 2]
-        return sums[:, :units], sums[:, units : 2 * units], squares
+    def squares_in(array):
+        terms = array[:, 2 * units : 2 * units + 2].astype(F32)
+        return terms[:, :1] + terms[:, 1:]
 
     handed = lax.ppermute(packed(*partial_sums(other)), CORE, [(0, 1), (1, 0)])
-    theirs = unpacked(handed.astype(F32))
-    blocks = packed(*[a + b for a, b in zip(partial_sums(core), theirs)])
+    gate, up, squares = lax.optimization_barrier(partial_sums(core))
+    gate = gate + handed[:, :units].astype(F32)
+    up = up + handed[:, units : 2 * units].astype(F32)
+    blocks = packed(gate, up, squares + squares_in(handed))
     blocks = exchange(blocks.reshape(-1, share, blocks.shape[1]), CHIPS)
-    gate_sum, up_sum, squares = unpacked(jnp.sum(blocks.astype(F32), axis=0))
+    sums = jnp.sum(blocks.astype(F32), axis=0)
+    gate_sum, up_sum, squares = sums[:, :units], sums[:, units : 2 * units], squares_in(sums)
     scale_rows = lax.rsqrt(squares / D + norm_eps)
     hidden = (jax.nn.silu(gate_sum * scale_rows) * (up_sum * scale_rows)).astype(BF16)
     hidden_full = collect_rows(hidden, FRAMES)

time: 194 us -> 193 us (level)
  no operation moved by 1% of the time
where the time goes in v5:
time: 193 us
  blocking collectives  167 us (87%)
  starting transfers between devices  9.24 us (5%)
  matrix products  5.73 us (3%)
  other arithmetic  5.47 us (3%)
  local copies, waits for them, and re-layouts  3.63 us (2%)
    all_to_all x7, blocking collectives, exchange(): return lax.all_to_all(blocks, axis, split_axis=0, concat_axis=0, tiled=True)  116 us
    all_gather x1, blocking collectives, gathered_features(): arrived = lax.all_gather(sent.reshape(-1, 8, LANES), 'heads', axis=0)  50.6 us
    all_to_all x1, starting transfers between devices, exchange(): return lax.all_to_all(blocks, axis, split_axis=0, concat_axis=0, tiled=True)  7.32 us
  transfers between devices with their start and end apart: 2, of which 1 were waited for; matrix products, arithmetic and copies ran while one was open for 3% of the time, Pallas kernels for 0%

profile of v5, /device:TPU:32, one launch (start us, length us, event | category | flops | bytes accessed | tf_op | source)
XLA Modules:
  0.0 192.7 jit_solution(14129064178734348130)
XLA Ops:
  0.0 1.3 convolution_convert_fusion.5
  1.3 0.7 broadcast_in_dim.11
  2.0 7.3 %all-to-all-start = ((bf16[32,8,256]{2,1,0:T(8,128)(2,1)}), bf16[32,8,256]{2,1,0:T(8,128)(2,1)S(1)}, u32[]{:S(2)}, u32[]{:S(2)}) async-start(bf16[32,8,256]{2,1,0:T(8,128)(2,1)} %broadcast_in_dim.11), calls=%async_computation | async-start | bytes 262144 | tf_op jit(solution)/shard_map/all_to_all | solution.py:21
  9.3 0.9 convert_bitcast_fusion.1
  10.3 0.6 abs_reduce_fusion
  11.8 50.6 %all-gather.1 = f16[16,73,8,128]{3,2,1,0:T(8,128)(2,1)S(1)} all-gather(f16[1,73,8,128]{3,2,1,0:T(8,128)(2,1)S(1)} %maximum_bitcast_fusion), channel_id=1, replica_groups=mesh['frames_0'=4,'frames_1'=4,'frames_2'=2,'heads'=16] {'heads'}, dimensions={0}, use_global_device_ids=true | all-gather | bytes 2541568 | tf_op jit(solution)/shard_map/all_gather | solution.py:88
  62.4 0.6 slice.83
  63.1 0.3 bitcast_convert_fusion
  63.4 1.0 fusion
  64.5 0.9 fusion.13
  65.5 0.9 fusion.10
  66.5 0.5 bitcast_reduce_fusion
  67.0 0.4 fusion.8
  67.3 0.5 fusion.16
  68.5 15.2 %all_to_all.40 = bf16[32,18,128]{2,1,0:T(8,128)(2,1)S(1)} all-to-all(bf16[32,18,128]{2,1,0:T(8,128)(2,1)S(1)} %pad_maximum_fusion.2), channel_id=1, replica_groups=mesh['frames_0'=4,'frames_1'=4,'frames_2'=2,'heads'=16] {'frames_0','fra..., dimensions={0} | all-to-all | bytes 294912 | tf_op jit(solution)/shard_map/all_to_all | solution.py:21
  84.7 11.4 %all_to_all.41 = bf16[32,8,256]{2,1,0:T(8,128)(2,1)S(1)} all-to-all(bf16[32,8,256]{2,1,0:T(8,128)(2,1)S(1)} %broadcast_in_dim.12), channel_id=1, replica_groups=mesh['frames_0'=4,'frames_1'=4,'frames_2'=2,'heads'=16] {'frames_0','fra..., dimensions={0} | all-to-all | bytes 262144 | tf_op jit(solution)/shard_map/all_to_all | solution.py:21
  96.3 22.1 %all_to_all.42 = bf16[16,16,256]{2,1,0:T(8,128)(2,1)S(1)} all-to-all(bf16[16,16,256]{2,1,0:T(8,128)(2,1)S(1)} %bitcast.139), channel_id=1, replica_groups=mesh['frames_0'=4,'frames_1'=4,'frames_2'=2,'heads'=16] {'heads'}, dimensions={0} | all-to-all | bytes 262144 | tf_op jit(solution)/shard_map/all_to_all | solution.py:21
  118.4 19.2 %all_to_all.43 = bf16[16,16,256]{2,1,0:T(8,128)(2,1)S(1)} all-to-all(bf16[16,16,256]{2,1,0:T(8,128)(2,1)S(1)} %broadcast_in_dim.13), channel_id=1, replica_groups=mesh['frames_0'=4,'frames_1'=4,'frames_2'=2,'heads'=16] {'heads'}, dimensions={0} | all-to-all | bytes 262144 | tf_op jit(solution)/shard_map/all_to_all | solution.py:21
  138.0 0.3 convolution_convert_fusion
  138.3 0.3 convolution_convert_fusion.1
  138.8 1.9 collective-permute-start
  140.9 0.2 fusion.35
  141.1 0.2 fusion.37
  141.3 0.2 copy.151
  141.5 0.2 copy.152
  141.7 0.9 collective-permute-done
  142.8 0.3 copy.153
  143.1 15.4 %all_to_all.44 = bf16[16,8,2176]{2,1,0:T(8,128)(2,1)S(1)} all-to-all(bf16[16,8,2176]{2,1,0:T(8,128)(2,1)S(1)} %bitcast.137), channel_id=1, replica_groups=mesh['frames_0'=4,'frames_1'=4,'frames_2'=2,'heads'=16] {'frames_0','fra..., dimensions={0} | all-to-all | bytes 1114112 | tf_op jit(solution)/shard_map/all_to_all | solution.py:21
  158.9 14.9 %all_to_all.45 = bf16[32,8,1024]{2,1,0:T(8,128)(2,1)S(1)} all-to-all(bf16[32,8,1024]{2,1,0:T(8,128)(2,1)S(1)} %broadcast_in_dim.14), channel_id=1, replica_groups=mesh['frames_0'=4,'frames_1'=4,'frames_2'=2,'heads'=16] {'frames_0','fra..., dimensions={0} | all-to-all | bytes 1048576 | tf_op jit(solution)/shard_map/all_to_all | solution.py:21
  173.9 0.3 convolution_convert_fusion.2
  174.2 17.9 %all_to_all.46 = bf16[16,16,256]{2,1,0:T(8,128)(2,1)S(1)} all-to-all(bf16[16,16,256]{2,1,0:T(8,128)(2,1)S(1)} %bitcast.140), channel_id=1, replica_groups=mesh['frames_0'=4,'frames_1'=4,'frames_2'=2,'heads'=16] {'heads'}, dimensions={0} | all-to-all | bytes 262144 | tf_op jit(solution)/shard_map/all_to_all | solution.py:21
  192.1 0.6 add_convert_fusion.2
  (76 shorter events, 3.5 us)
Async XLA Ops:
  0.0 64.4 %copy-start = (bf16[1152,256]{1,0:T(8,128)(2,1)S(1)}, bf16[1152,256]{1,0:T(8,128)(2,1)}, u32[]{:S(2)}) copy-start(bf16[1152,256]{1,0:T(8,128)(2,1)} %param.13) | copy-start | bytes 1769476
  2.0 64.4 %all-to-all-start = ((bf16[32,8,256]{2,1,0:T(8,128)(2,1)}), bf16[32,8,256]{2,1,0:T(8,128)(2,1)S(1)}, u32[]{:S(2)}, u32[]{:S(2)}) async-start(bf16[32,8,256]{2,1,0:T(8,128)(2,1)} %broadcast_in_dim.11), calls=%async_computation | async-start | bytes 262144 | tf_op jit(solution)/shard_map/all_to_all | solution.py:21
  64.4 1.1 copy-start.6
  67.3 28.8 %copy-start.4 = (bf16[256,256]{1,0:T(8,128)(2,1)S(1)}, bf16[256,256]{1,0:T(8,128)(2,1)}, u32[]{:S(2)}) copy-start(bf16[256,256]{1,0:T(8,128)(2,1)} %param.15) | copy-start | bytes 393220
  67.9 70.1 %copy-start.5 = (f32[256]{0:T(256)S(1)}, f32[256]{0:T(256)}, u32[]{:S(2)}) copy-start(f32[256]{0:T(256)} %param.16) | copy-start | bytes 3076
  67.9 70.1 %copy-start.1 = (bf16[256,1024]{1,0:T(8,128)(2,1)S(1)}, bf16[256,1024]{1,0:T(8,128)(2,1)}, u32[]{:S(2)}) copy-start(bf16[256,1024]{1,0:T(8,128)(2,1)} %param.18) | copy-start | bytes 1572868
  68.4 69.9 %copy-start.2 = (bf16[256,1024]{1,0:T(8,128)(2,1)S(1)}, bf16[256,1024]{1,0:T(8,128)(2,1)}, u32[]{:S(2)}) copy-start(bf16[256,1024]{1,0:T(8,128)(2,1)} %param.17) | copy-start | bytes 1572868
  138.8 3.9 %collective-permute-start = (bf16[128,2176]{0,1:T(8,128)(2,1)S(1)}, bf16[128,2176]{0,1:T(8,128)(2,1)S(1)}, u32[]{:S(2)}, u32[]{:S(2)}) collective-permute-start(bf16[128,2176]{0,1:T(8,128)(2,1)S(1)} %pad_maximum_fusion), channel_id=1, source_target_pairs={{0,16},{16,0},{1,17},{17,1},{2,18},{18,2},{3,19},{19,3},{4,20},{20... | collective-permute-start | bytes 1671176 | tf_op jit(solution)/shard_map/ppermute | solution.py:146
  142.8 31.1 %copy-start.3 = (bf16[1024,256]{1,0:T(8,128)(2,1)S(1)}, bf16[1024,256]{1,0:T(8,128)(2,1)}, u32[]{:S(2)}) copy-start(bf16[1024,256]{1,0:T(8,128)(2,1)} %param.19) | copy-start | bytes 1572868
